TPU v7x, 32 devices: a whole 2x2x4 slice. The times are simulated.
32 devices in a mesh: rep: 2 (over x), exp: 2 (over core), tp: 8 (over z, y).
Axes of the slice: x: 2, y: 2, z: 4, core: 2. Of those that a mesh axis runs over, the one named last changes fastest.
Arguments:
- tokens: bfloat16 [1024, 4096], P(('rep', 'exp'), 'tp'), parts along dimension 0
- smooth_in: float32 [4096], P('tp'), may hold values from 0.5 to 2
- expert_ids: int32 [1024, 2], P(('rep', 'exp')), parts along dimension 0, may hold values from 0 to 3, as said below
- gate_fixed: int32 [1024, 2], P(('rep', 'exp')), parts along dimension 0, may hold values from 1 to 32767
- slots: int32 [1024, 2], P(('rep', 'exp')), parts along dimension 0, may hold values from 0 to 255, as said below
- w_gate: bfloat16 [4, 4096, 7168], P('exp', None, 'tp')
- w_up: bfloat16 [4, 4096, 7168], P('exp', None, 'tp')
- w_down: bfloat16 [4, 7168, 4096], P('exp', 'tp')
- gate_scale: float32 [4, 7168], P('exp', 'tp'), may hold values from 0.00010557433 to 0.0004222973
- up_scale: float32 [4, 7168], P('exp', 'tp'), may hold values from 0.00010557433 to 0.0004222973
- smooth_mid: float32 [4, 7168], P('exp', 'tp'), may hold values from 0.5 to 2
- down_scale: float32 [4, 4096], P('exp'), may hold values from 0.00015961338 to 0.0006384535
Outputs:
- moe_out: bfloat16 [1024, 4096], P(('rep', 'exp'), 'tp'), parts along dimension 0
There are 2 independent parts, one for each index of `rep`. A program takes and returns all parts, laid end to end along the dimension named above; an argument that names none is the same for every part. Nothing has to cross between parts.
Inputs may be any that keep to these rules, and one draw needn't show every extreme that they name: `expert_ids`: the two experts of a token differ. Within one aligned block of 256 tokens (the tokens of one index of exp), the slots of the pairs that name one expert are distinct and run from 0 to their number less one. In every block some expert is named by 192 or more tokens.
All inputs are finite; a program needn't handle non-finite values.
Results may differ from a plain program's by a relative error of at most 0.006.
Values may be sent and summed in bfloat16 or wider, within the bound.
A program may use at most 128 MiB of HBM per device.

v0:
```python
import jax
import jax.numpy as jnp
from jax import lax
from jax.sharding import PartitionSpec as P

CLIP_RATIO = 0.35
EPSILON = 1e-06


def per_device(
    tokens,
    smooth_in,
    expert_ids,
    gate_fixed,
    slots,
    w_gate,
    w_up,
    w_down,
    gate_scale,
    up_scale,
    smooth_mid,
    down_scale,
):
    n_groups = lax.axis_size("exp")
    local_experts = w_gate.shape[0]
    block_rows = tokens.shape[0]
    capacity = 3 * block_rows // 4
    rows_all = local_experts * n_groups * capacity
    smoothed = tokens.astype(jnp.float32) / smooth_in[None, :]
    local_peak = jnp.max(jnp.abs(smoothed), axis=1)
    row_peak_value = lax.pmax(local_peak, "tp")
    in_scale = CLIP_RATIO * (row_peak_value + EPSILON) / 127.0
    quantized = jnp.clip(smoothed / in_scale[:, None], -127.0, 127.0).astype(jnp.bfloat16)
    gate_values = gate_fixed.astype(jnp.float32)
    weight = gate_values / jnp.sum(gate_values, axis=1, keepdims=True)
    kept_pairs = slots < capacity
    target = expert_ids * capacity + jnp.minimum(slots, capacity - 1)
    positions = jnp.arange(rows_all, dtype=jnp.int32)
    place_first = (target[:, 0][None, :] == positions[:, None]) & kept_pairs[:, 0][None, :]
    place_second = (target[:, 1][None, :] == positions[:, None]) & kept_pairs[:, 1][None, :]
    placement_map = place_first | place_second
    send_rows = jnp.dot(
        placement_map.astype(jnp.bfloat16), quantized, preferred_element_type=jnp.float32
    ).astype(jnp.bfloat16)
    send_rows = send_rows.reshape(n_groups, local_experts, capacity, tokens.shape[1])
    scale_slots = jnp.sum(jnp.where(placement_map, in_scale[None, :], 0.0), axis=1).reshape(
        n_groups, local_experts, capacity
    )
    recv_rows = lax.all_to_all(send_rows, "exp", split_axis=0, concat_axis=0, tiled=True)
    recv_scale = lax.all_to_all(scale_slots, "exp", split_axis=0, concat_axis=0, tiled=True)
    arrived = lax.all_gather(recv_rows, "tp", axis=3, tiled=True)
    gate_more = jnp.einsum("secl,elf->secf", arrived, w_gate, preferred_element_type=jnp.float32)
    up_more = jnp.einsum("secl,elf->secf", arrived, w_up, preferred_element_type=jnp.float32)
    gate_pre = gate_more * recv_scale[..., None] * gate_scale[None, :, None, :]
    up_pre = up_more * recv_scale[..., None] * up_scale[None, :, None, :]
    hidden = jax.nn.silu(gate_pre) * up_pre / smooth_mid[None, :, None, :]
    hidden_max = lax.pmax(jnp.max(jnp.abs(hidden), axis=3), "tp")
    mid_scale = CLIP_RATIO * (hidden_max + EPSILON) / 127.0
    hidden_q = jnp.clip(hidden / mid_scale[..., None], -127.0, 127.0).astype(jnp.bfloat16)
    down_acc = jnp.einsum("secf,efd->secd", hidden_q, w_down, preferred_element_type=jnp.float32)
    partial_value = down_acc * mid_scale[..., None] * down_scale[None, :, None, :]
    summed = lax.psum_scatter(partial_value, "tp", scatter_dimension=3, tiled=True)
    returned = lax.all_to_all(summed, "exp", split_axis=0, concat_axis=0, tiled=True)
    slot_table = returned.reshape(rows_all, returned.shape[3])
    picked = jnp.take(slot_table, target, axis=0)
    pair_weight = jnp.where(kept_pairs, weight, 0.0)
    combined = jnp.sum(picked * pair_weight[:, :, None], axis=1)
    return combined.astype(jnp.bfloat16)


def solution(mesh):
    in_specs = (
        P(("rep", "exp"), "tp"),
        P("tp"),
        P(("rep", "exp"), None),
        P(("rep", "exp"), None),
        P(("rep", "exp"), None),
        P("exp", None, "tp"),
        P("exp", None, "tp"),
        P("exp", "tp", None),
        P("exp", "tp"),
        P("exp", "tp"),
        P("exp", "tp"),
        P("exp", None),
    )
    out_specs = P(("rep", "exp"), "tp")
    return jax.shard_map(
        per_device, mesh=mesh, in_specs=in_specs, out_specs=out_specs, check_vma=False
    )
```

profile of v0, /device:TPU:0, one launch (start us, length us, event | category | flops | bytes accessed | tf_op | source)
XLA Modules:
  0.0 419.6 jit_solution(16711710052682556564)
XLA Ops:
  6.5 0.0 all-gather.2.cloned.1.call-start
  6.5 0.7 compare_and_fusion
  7.3 0.7 convert_reduce_fusion
  8.0 0.7 divide_select_fusion
  8.7 1.1 fusion.24
  9.8 23.2 %pmax.14 = f32[256]{0:T(256)S(1)} all-reduce(f32[256]{0:T(256)S(1)} %fusion.24), channel_id=1, replica_groups=mesh['rep'=2,'exp'=2,'tp'=8] {'tp'}, use_global_device_ids=true, to_apply=%region_1.0 | all-reduce | flops 256 | bytes 2048 | tf_op jit(solution)/shard_map/pmax | solution.py:31
  33.0 1.5 convolution_convert_fusion
  34.5 4.4 %all_to_all.15 = bf16[2,2,192,512]{3,2,1,0:T(8,128)(2,1)S(1)} all-to-all(bf16[2,2,192,512]{3,2,1,0:T(8,128)(2,1)S(1)} %bitcast.44), channel_id=1, replica_groups=mesh['rep'=2,'exp'=2,'tp'=8] {'exp'}, dimensions={0} | all-to-all | bytes 1572864 | tf_op jit(solution)/shard_map/all_to_all | solution.py:49
  38.8 0.9 copy.29
  39.8 0.0 all-gather.2.cloned.1.call-update
  39.8 0.0 reduce-scatter.2.cloned.1.call-start
  39.8 0.3 select_reduce_fusion
  40.2 0.1 reshape.30
  40.3 3.7 all_to_all.16
  43.9 0.0 copy-start.2
  43.9 0.0 copy-start.3
  44.0 0.0 copy-start.4
  44.0 92.7 %all-gather.2.cloned.1.call-done = bf16[2,2,192,4096]{3,2,0,1:T(8,128)(2,1)} async-done(((bf16[2,2,192,512]{3,2,0,1:T(8,128)(2,1)}), bf16[2,2,192,4096]{3,2,0,1:T(8,128)(2,1)}) %all-gather.2.cloned.1.call-update) | async-done | bytes 6291472 | tf_op jit(solution)/shard_map/all_gather | solution.py:51
  136.7 0.0 copy-start
  136.7 14.6 %fusion.2 = f32[2,2,192,896]{3,2,1,0:T(8,128)S(1)} fusion(bf16[2,2,192,4096]{3,2,0,1:T(8,128)(2,1)} %all-gather.2.cloned.1.call-done, bf16[2,4096,896]{2,1,0:T(8,128)(2,1)} %param.18), kind=kOutput, calls=%fused_computation.3 | convolution fusion | flops 5637144576 | bytes 23724032 | tf_op jit(solution)/shard_map/secl,elf->secf/dot_general | solution.py:53
  151.3 0.0 copy-done.2
  151.3 0.0 copy-done.3
  151.3 0.0 copy-done.4
  151.3 0.0 copy-done
  151.3 0.0 copy-start.1
  151.3 10.8 %abs_reduce_fusion = (f32[2,2,192]{2,0,1:T(2,128)S(1)}, f32[2,2,192,896]{3,2,0,1:T(8,128)S(1)}) fusion(f32[2,896]{1,0:T(2,128)S(1)} %copy-done.4, f32[2,896]{1,0:T(2,128)S(1)} %copy-done.2, f32[2,2,192,896]{3,2,1,0:T(8,128)S(1)} %fusion.2, f32[2,896]{1,0:T(2,128)S(1)} %copy-done.3, f32[2,2,192]{2,0,1:T(2,128)S(1)} %copy.30, ...), kind=kOutput, calls=%fused_computation.15 | convolution fusion | flops 5645401088 | bytes 26504192 | tf_op jit(solution)/shard_map/secl,elf->secf/dot_general | solution.py:52
  162.2 18.8 %pmax.15 = f32[2,2,192]{2,0,1:T(2,128)S(1)} all-reduce(f32[2,2,192]{2,0,1:T(2,128)S(1)} %get-tuple-element.13), channel_id=1, replica_groups=mesh['rep'=2,'exp'=2,'tp'=8] {'tp'}, use_global_device_ids=true, to_apply=%region_4.5 | all-reduce | flops 768 | bytes 6144 | tf_op jit(solution)/shard_map/pmax | solution.py:57
  181.0 0.0 copy-done.1
  181.0 14.8 %fusion.6 = f32[2,2,192,4096]{3,2,0,1:T(8,128)} fusion(bf16[2,896,4096]{2,1,0:T(8,128)(2,1)} %param.19, f32[2,4096]{1,0:T(2,128)S(1)} %copy-done.1, f32[2,2,192]{2,0,1:T(2,128)S(1)} %add_multiply_fusion, f32[2,2,192,896]{3,2,0,1:T(8,128)S(1)} %get-tuple-element.14, f32[2,896]{1,0:T(2,128)S(1)} %copy-done.4), kind=kOutput, calls=%fused_computation.8 | convolution fusion | flops 5646188544 | bytes 30058496 | tf_op jit(solution)/shard_map/secf,efd->secd/dot_general | solution.py:60
  195.8 0.0 reduce-scatter.2.cloned.1.call-update
  195.8 0.1 copy.32
  196.0 0.1 reshape.34
  196.1 0.1 copy.33
  196.2 0.2 copy.28
  196.4 204.7 %reduce-scatter.2.cloned.1.call-done = f32[2,2,192,512]{3,2,0,1:T(8,128)} async-done(((f32[2,2,192,4096]{3,2,0,1:T(8,128)}), f32[2,2,192,512]{3,2,0,1:T(8,128)}) %reduce-scatter.2.cloned.1.call-update) | async-done | bytes 1572880 | tf_op jit(solution)/shard_map/reduce_scatter | solution.py:62
  401.1 1.5 copy.31
  402.6 5.0 %all_to_all.17 = f32[2,2,192,512]{3,2,1,0:T(8,128)S(1)} all-to-all(f32[2,2,192,512]{3,2,1,0:T(8,128)S(1)} %copy.31), channel_id=1, replica_groups=mesh['rep'=2,'exp'=2,'tp'=8] {'exp'}, dimensions={0} | all-to-all | bytes 3145728 | tf_op jit(solution)/shard_map/all_to_all | solution.py:63
  407.6 1.6 gather_fusion
  409.3 0.6 reshape.33
  409.9 2.9 multiply_reduce_fusion
  (7 shorter events, 0.1 us)
Async XLA Ops:
  6.5 130.1 %all-gather.2.cloned.1.call-start = ((), (), s32[]{:S(2)}) async-start(), calls=%async_computation.4 | async-start | bytes 7077888 | tf_op jit(solution)/shard_map/all_gather | solution.py:51
  39.8 361.3 %reduce-scatter.2.cloned.1.call-start = ((), (), s32[]{:S(2)}) async-start(), calls=%async_computation.5 | async-start | bytes 14155776 | tf_op jit(solution)/shard_map/reduce_scatter | solution.py:62
  43.9 107.3 %copy-start.2 = (f32[2,896]{1,0:T(2,128)S(1)}, f32[2,896]{1,0:T(2,128)}, u32[]{:S(2)}) copy-start(f32[2,896]{1,0:T(2,128)} %param.21) | copy-start | bytes 21508
  43.9 107.4 %copy-start.3 = (f32[2,896]{1,0:T(2,128)S(1)}, f32[2,896]{1,0:T(2,128)}, u32[]{:S(2)}) copy-start(f32[2,896]{1,0:T(2,128)} %param.20) | copy-start | bytes 21508
  44.0 107.4 %copy-start.4 = (f32[2,896]{1,0:T(2,128)S(1)}, f32[2,896]{1,0:T(2,128)}, u32[]{:S(2)}) copy-start(f32[2,896]{1,0:T(2,128)} %param.22) | copy-start | bytes 21508
  136.7 14.6 %copy-start = (bf16[2,2,192,4096]{3,2,0,1:T(8,128)(2,1)S(1)}, bf16[2,2,192,4096]{3,2,0,1:T(8,128)(2,1)}, u32[]{:S(2)}) copy-start(bf16[2,2,192,4096]{3,2,0,1:T(8,128)(2,1)} %all-gather.2.cloned.1.call-done) | copy-start | bytes 18874372
  151.3 29.6 %copy-start.1 = (f32[2,4096]{1,0:T(2,128)S(1)}, f32[2,4096]{1,0:T(2,128)}, u32[]{:S(2)}) copy-start(f32[2,4096]{1,0:T(2,128)} %param.23) | copy-start | bytes 98308
Sparse Core Ops, SparseCore 0:
  39.9 96.7 all-gather.1
  195.9 205.1 reduce-scatter.1
where the time goes:
time: 420 us
  waiting for transfers between devices  297 us (71%)
  blocking collectives  55 us (13%)
  matrix products  41.7 us (10%)
  between operations  13.6 us (3%)
  other arithmetic  6.44 us (2%)
  local copies, waits for them, and re-layouts  5.43 us (1%)
    reduce_scatter x1, waiting for transfers between devices, per_device(): lax.psum_scatter(partial_value, 'tp', scatter_dimension=3, tiled=True)  205 us
    all_gather x1, waiting for transfers between devices, per_device(): arrived = lax.all_gather(recv_rows, 'tp', axis=3, tiled=True)  92.7 us
    pmax x1, blocking collectives, per_device(): row_peak_value = lax.pmax(local_peak, 'tp')  23.2 us
    pmax x1, blocking collectives, per_device(): hidden_max = lax.pmax(jnp.max(jnp.abs(hidden), axis=3), 'tp')  18.8 us
    dot_general x1, matrix products, per_device(): jnp.einsum('secf,efd->secd', hidden_q, w_down, preferred_element_type=jnp...  14.8 us
    dot_general x1, matrix products, per_device(): jnp.einsum('secl,elf->secf', arrived, w_up, preferred_element_type=jnp.fl...  14.6 us
    dot_general x1, matrix products, per_device(): jnp.einsum('secl,elf->secf', arrived, w_gate, preferred_element_type=jnp....  10.8 us
  transfers between devices with their start and end apart: 2, of which 2 were waited for; matrix products, arithmetic and copies ran while one was open for 0% of the time, Pallas kernels for 0%

commit v1 on v0

v1 whole, which is shorter than its diff:
```python
import functools

import jax
import jax.numpy as jnp
from jax import lax
from jax.experimental import pallas as pl
from jax.experimental.pallas import tpu as pltpu
from jax.sharding import PartitionSpec as P

CLIP_RATIO = 0.35
EPSILON = 1e-06
LANES = 128
MESH = pl.DeviceIdType.MESH
F32 = jnp.float32
BF16 = jnp.bfloat16


def kernel(
    n, slots,
    tok_ref, smooth_ref, share_ref, wg_ref, wu_ref, wd_ref, gs_ref, us_ref, sm_ref, ds_ref,
    out_ref,
    x, wbuf, dbuf, acc, hq, meta, coef, pk, hx, hm, own, ssend, srecv, ysend, yrecv, comb, zsend, zrecv,
    w_sem, d_sem, pk_s, pk_r, hx_s, hx_r, meta_s, meta_r,
    az_s, ay_s, as_s, ag_r, as_r, rs_s, rs_r, ry_s, ry_r, rz_s, rz_r,
):
    q = n // 2
    me = lax.axis_index("tp")
    core = lax.axis_index("exp")
    z, y = me // 2, me % 2
    direction = 1 - 2 * (z % 2)
    experts = wg_ref.shape[0]
    block, depth = tok_ref.shape
    width = wg_ref.shape[2]

    def z_of(j):
        return (z + direction * j + q) % q

    def chunk(j, other):
        row = y + other * (1 - 2 * y)
        return z_of(j) * 2 + row

    def remote(src, dst, send, recv, device):
        return pltpu.make_async_remote_copy(
            src_ref=src, dst_ref=dst, send_sem=send, recv_sem=recv,
            device_id=device, device_id_type=MESH,
        )

    sibling = {"exp": 1 - core}
    partner = {"tp": chunk(0, 1)}

    def weight_copies(k):
        rows = pl.ds(pl.multiple_of(chunk(k // 2, k % 2) * depth, depth), depth)
        slot = k % slots
        return [
            pltpu.make_async_copy(ref.at[:, rows, :], wbuf.at[slot, i], w_sem.at[slot, i])
            for i, ref in enumerate((wg_ref, wu_ref))
        ]

    def down_copy(p):
        cols = pl.ds(pl.multiple_of(p * depth, depth), depth)
        return pltpu.make_async_copy(wd_ref.at[:, :, cols], dbuf.at[p], d_sem.at[p])

    for k in range(slots):
        for copy in weight_copies(k):
            copy.start()

    barrier = pltpu.get_barrier_semaphore()
    pl.semaphore_signal(barrier, inc=1, device_id=sibling, device_id_type=MESH)

    @pl.loop(1, n)
    def _(d):
        pl.semaphore_signal(barrier, inc=1, device_id={"tp": (me + d) % n}, device_id_type=MESH)

    smoothed = tok_ref[...].astype(F32) / smooth_ref[...]
    peak = jnp.max(jnp.abs(smoothed), axis=1, keepdims=True)
    peak_row = jnp.broadcast_to(peak, (block, LANES)).T[0:1, :]
    pk[pl.ds(me, 1)] = peak_row[None]

    pl.semaphore_wait(barrier, n)

    def pk_copy(d):
        return remote(pk.at[me], pk.at[me], pk_s.at[d], pk_r.at[me], {"tp": (me + d) % n})

    @pl.loop(1, n)
    def _(d):
        pk_copy(d).start()

    @pl.loop(0, 2 * experts)
    def _(t):
        acc[t] = jnp.zeros(acc.shape[1:], F32)

    @pl.loop(1, n)
    def _(d):
        p = (me + d) % n
        remote(pk.at[p], pk.at[p], pk_s.at[d], pk_r.at[p], {"tp": p}).wait_recv()

    row_peak = jnp.max(pk[0:n], axis=0)
    peak_col = jnp.broadcast_to(row_peak, (LANES, block)).T
    in_scale = CLIP_RATIO * (peak_col + EPSILON) / 127.0
    smoothed = tok_ref[...].astype(F32) / smooth_ref[...]
    x[me, core] = jnp.clip(smoothed / in_scale[:, 0:1], -127.0, 127.0).astype(BF16)
    lane = lax.broadcasted_iota(jnp.int32, (block, LANES), 1)
    meta[core] = jnp.where(lane < 2 * experts, share_ref[...], in_scale)

    def z_copy(j):
        return remote(x.at[me, core], x.at[me, core], az_s.at[j], ag_r.at[me], {"tp": chunk(j, 0)})

    def y_copy(j):
        p = chunk(j, 0)
        return remote(x.at[p, core], x.at[p, core], ay_s.at[j], ag_r.at[p], partner)

    def sib_copy(p, b):
        return remote(x.at[p, b], x.at[p, b], as_s.at[p], as_r.at[p], sibling)

    def arrived(p):
        remote(x.at[p, core], x.at[p, core], as_s.at[p], ag_r.at[p], sibling).wait_recv()

    y_copy(0).start()

    @pl.loop(1, q)
    def _(j):
        z_copy(j).start()

    meta_copy = remote(meta.at[core], meta.at[core], meta_s, meta_r, sibling)
    meta_copy.start()
    sib_copy(me, core).start()

    def compute(k):
        p = chunk(k // 2, k % 2)
        slot = k % slots
        for copy in weight_copies(k):
            copy.wait()
        sib_copy(p, 1 - core).wait_recv()

        @pl.loop(0, 2 * experts)
        def _(t):
            acc[t] += jnp.dot(
                x[p].reshape(2 * block, depth), wbuf[slot, t // experts, t % experts],
                preferred_element_type=F32,
            )

        @pl.when(k + slots < n)
        def _():
            for copy in weight_copies(k + slots):
                copy.start()

        down_copy(p).start()

    compute(0)
    arrived(chunk(0, 1))
    sib_copy(chunk(0, 1), core).start()

    @pl.loop(1, q)
    def _(j):
        p = chunk(j, 0)
        arrived(p)
        y_copy(j).start()
        sib_copy(p, core).start()
        compute(2 * j - 1)
        compute(2 * j)
        p = chunk(j, 1)
        arrived(p)
        sib_copy(p, core).start()

    compute(n - 1)
    meta_copy.wait_recv()

    rb = 32
    blocks = block // rb
    for e in range(experts):

        @pl.loop(0, 2 * blocks)
        def _(r):
            rows = pl.ds(pl.multiple_of(r * rb, rb), rb)
            inner = pl.ds(pl.multiple_of((r % blocks) * rb, rb), rb)
            scale = meta[r // blocks, inner, :][:, LANES - 1:]
            gate = acc[e, rows, :] * scale * gs_ref[...][e:e + 1]
            up = acc[experts + e, rows, :] * scale * us_ref[...][e:e + 1]
            hidden = gate / (1.0 + jnp.exp(-gate)) * up / sm_ref[...][e:e + 1]
            acc[e, rows, :] = hidden
            hm[rows, :] = jnp.broadcast_to(jnp.max(jnp.abs(hidden), axis=1, keepdims=True), (rb, LANES))

        hx[pl.ds(me, 1), e:e + 1, :] = hm[...].T[0:1, :][None]

    def hx_copy(d):
        return remote(hx.at[me], hx.at[me], hx_s.at[d], hx_r.at[me], {"tp": (me + d) % n})

    @pl.loop(1, n)
    def _(d):
        hx_copy(d).start()

    @pl.loop(1, n)
    def _(d):
        p = (me + d) % n
        remote(hx.at[p], hx.at[p], hx_s.at[d], hx_r.at[p], {"tp": p}).wait_recv()

    mid_rows = CLIP_RATIO * (jnp.max(hx[0:n], axis=0) + EPSILON) / 127.0
    for e in range(experts):
        coef[e] = jnp.broadcast_to(mid_rows[e:e + 1, :], (LANES, 2 * block)).T

        @pl.loop(0, 2 * blocks)
        def _(r):
            rows = pl.ds(pl.multiple_of(r * rb, rb), rb)
            inner = pl.ds(pl.multiple_of((r % blocks) * rb, rb), rb)
            mid = coef[e, rows, :]
            hq[e, rows, :] = jnp.clip(acc[e, rows, :] * (1.0 / mid[:, 0:1]), -127.0, 127.0).astype(BF16)
            lanes = lax.broadcasted_iota(jnp.int32, (rb, LANES), 1)
            picked = jnp.where(lanes == core * experts + e, meta[r // blocks, inner, :], 0.0)
            coef[e, rows, :] = mid * jnp.sum(picked, axis=1, keepdims=True)

    def partial(p, b):
        rows = pl.ds(pl.multiple_of(b * block, block), block)
        cols = pl.ds(pl.multiple_of(p * depth, depth), depth)
        total = None
        for e in range(experts):
            part = jnp.dot(hq[e, rows, :], dbuf[p, e], preferred_element_type=F32)
            part = part * coef[e, rows, 0:1] * ds_ref[:, cols][e:e + 1]
            total = part if total is None else total + part
        return total

    def shard_of(k):
        return chunk(q - 1 - k % q, 1 - k // q)

    def rs_copy(k):
        return remote(ssend.at[k], srecv.at[k], rs_s.at[k], rs_r.at[k], sibling)

    def ry_copy(j):
        return remote(ysend.at[j], yrecv.at[j], ry_s.at[j], ry_r.at[j], partner)

    def rz_copy(j):
        return remote(zsend.at[j], zrecv.at[z], rz_s.at[j], rz_r.at[z], {"tp": chunk(j, 0)})

    def combine(k):
        j = q - 1 - k % q
        rs_copy(k).wait_recv()

        @pl.when(k < q)
        def _():
            ysend[j] = (own[k % 2] + srecv[k].astype(F32)).astype(BF16)
            ry_copy(j).start()

        @pl.when(k >= q)
        def _():
            comb[j] = own[k % 2] + srecv[k].astype(F32)

    @pl.loop(0, n)
    def _(k):
        p = shard_of(k)
        down_copy(p).wait()
        ssend[k] = partial(p, 1 - core).astype(BF16)
        rs_copy(k).start()
        own[k % 2] = partial(p, core)

        @pl.when(k > 0)
        def _():
            combine(k - 1)

    combine(n - 1)

    @pl.loop(0, q - 1)
    def _(i):
        j = q - 1 - i
        ry_copy(j).wait_recv()
        zsend[j] = (comb[j] + yrecv[j].astype(F32)).astype(BF16)
        rz_copy(j).start()

    ry_copy(0).wait_recv()
    comb[0] += yrecv[0].astype(F32)

    @pl.loop(1, q)
    def _(j):
        s = z_of(j)
        remote(zsend.at[j], zrecv.at[s], rz_s.at[j], rz_r.at[s], sibling).wait_recv()
        comb[0] += zrecv[s].astype(F32)

    out_ref[...] = comb[0].astype(BF16)

    meta_copy.wait_send()

    @pl.loop(1, n)
    def _(d):
        pk_copy(d).wait_send()
        hx_copy(d).wait_send()

    @pl.loop(0, n)
    def _(k):
        sib_copy(k, core).wait_send()
        rs_copy(k).wait_send()

    @pl.loop(0, q)
    def _(j):
        y_copy(j).wait_send()
        ry_copy(j).wait_send()

    @pl.loop(1, q)
    def _(j):
        z_copy(j).wait_send()
        rz_copy(j).wait_send()


def per_device(
    n,
    tokens, smooth_in, expert_ids, gate_fixed, slots,
    w_gate, w_up, w_down, gate_scale, up_scale, smooth_mid, down_scale,
):
    q = n // 2
    experts, _, width = w_gate.shape
    block, depth = tokens.shape
    capacity = 3 * block // 4
    gate_values = gate_fixed.astype(F32)
    weight = gate_values / jnp.sum(gate_values, axis=1, keepdims=True)
    pair_weight = jnp.where(slots < capacity, weight, 0.0)
    lane = jnp.arange(LANES, dtype=jnp.int32)[None, :]
    share = sum(
        jnp.where(expert_ids[:, k:k + 1] == lane, pair_weight[:, k:k + 1], 0.0)
        for k in range(expert_ids.shape[1])
    )
    ring = min(n, 5)
    vmem = pl.BlockSpec(memory_space=pltpu.VMEM)
    hbm = pl.BlockSpec(memory_space=pl.ANY)
    dma = pltpu.SemaphoreType.DMA
    slab = (block, depth)
    return pl.pallas_call(
        functools.partial(kernel, n, ring),
        out_shape=jax.ShapeDtypeStruct(slab, BF16),
        in_specs=[vmem] * 3 + [hbm] * 3 + [vmem] * 4,
        out_specs=vmem,
        scratch_shapes=[
            pltpu.VMEM((n, 2, *slab), BF16),
            pltpu.VMEM((ring, 2, experts, depth, width), BF16),
            pltpu.VMEM((n, experts, width, depth), BF16),
            pltpu.VMEM((2 * experts, 2 * block, width), F32),
            pltpu.VMEM((experts, 2 * block, width), BF16),
            pltpu.VMEM((2, block, LANES), F32),
            pltpu.VMEM((experts, 2 * block, LANES), F32),
            pltpu.VMEM((n + 8, 1, block), F32),
            pltpu.VMEM((n + 8, experts, 2 * block), F32),
            pltpu.VMEM((2 * block, LANES), F32),
            pltpu.VMEM((2, *slab), F32),
            pltpu.VMEM((n, *slab), BF16),
            pltpu.VMEM((n, *slab), BF16),
            pltpu.VMEM((q, *slab), BF16),
            pltpu.VMEM((q, *slab), BF16),
            pltpu.VMEM((q, *slab), F32),
            pltpu.VMEM((q, *slab), BF16),
            pltpu.VMEM((q, *slab), BF16),
            dma((ring, 2)), dma((n,)), dma((n,)), dma((n,)), dma((n,)), dma((n,)), dma, dma,
            dma((q,)), dma((q,)), dma((n,)), dma((n,)), dma((n,)),
            dma((n,)), dma((n,)), dma((q,)), dma((q,)), dma((q,)), dma((q,)),
        ],
        compiler_params=pltpu.CompilerParams(
            collective_id=0, has_side_effects=True, vmem_limit_bytes=67043328
        ),
    )(tokens, smooth_in[None, :], share, w_gate, w_up, w_down, gate_scale, up_scale, smooth_mid, down_scale)


def solution(mesh):
    n = mesh.shape["tp"]
    in_specs = (
        P(("rep", "exp"), "tp"),
        P("tp"),
        P(("rep", "exp"), None),
        P(("rep", "exp"), None),
        P(("rep", "exp"), None),
        P("exp", None, "tp"),
        P("exp", None, "tp"),
        P("exp", "tp", None),
        P("exp", "tp"),
        P("exp", "tp"),
        P("exp", "tp"),
        P("exp", None),
    )
    out_specs = P(("rep", "exp"), "tp")
    return jax.shard_map(
        functools.partial(per_device, n), mesh=mesh, in_specs=in_specs, out_specs=out_specs, check_vma=False
    )
```

time: 420 us -> 107 us (0.25)
  waiting for transfers between devices: 297 us -> 0 us
  Pallas kernels: 0 us -> 102 us
  blocking collectives: 55 us -> 0 us
  matrix products: 41.7 us -> 0 us
  between operations: 13.6 us -> 0.01 us
    reduce_scatter x1 -> x0, waiting for transfers between devices: 205 us -> none  [per_device(): lax.psum_scatter(partial_value, 'tp', scatter_dimension=3, tiled=True)]
    pallas_call x0 -> x1, Pallas kernels: none -> 102 us  [per_device(): pl.pallas_call(functools.partial(kernel, n, ring), out_shape=jax.ShapeDty...]
    all_gather x1 -> x0, waiting for transfers between devices: 92.7 us -> none  [per_device(): arrived = lax.all_gather(recv_rows, 'tp', axis=3, tiled=True)]
    pmax x2 -> x0, blocking collectives: 41.9 us -> none  [the longest x1 23.2 us: per_device(): row_peak_value = lax.pmax(local_peak, 'tp')]
    dot_general x4 -> x0, matrix products: 41.7 us -> none  [the longest x1 14.8 us: per_device(): jnp.einsum('secf,efd->secd', hidden_q, w_down, preferred_element_type=jnp...]
    all_to_all x3 -> x0, blocking collectives: 13.1 us -> none  [the longest x1 5 us: per_device(): lax.all_to_all(summed, 'exp', split_axis=0, concat_axis=0, tiled=True)]
  transfers between devices with their start and end apart: 2 -> 0, of which waited for: 2 -> 0; matrix products, arithmetic and copies ran while one was open for 0% -> 0% of each run, Pallas kernels for 0% -> 0%
where the time goes in v1:
time: 107 us; the launch traced here: 106 us
  Pallas kernels  102 us (95%)
  local copies, waits for them, and re-layouts  2.44 us (2%)
  other arithmetic  2.26 us (2%)
    pallas_call x1, Pallas kernels, per_device(): pl.pallas_call(functools.partial(kernel, n, ring), out_shape=jax.ShapeDty...  102 us

profile of v1, /device:TPU:0, one launch (start us, length us, event | category | flops | bytes accessed | tf_op | source)
XLA Modules:
  0.0 106.3 jit_solution(6233028246580393184)
XLA Ops:
  0.0 0.7 convert_reduce_fusion
  0.7 0.7 compare_select_fusion
  1.4 0.8 fusion
  2.2 0.9 select_add_fusion.share_ref
  3.0 101.6 %shard_map.118 = bf16[256,512]{1,0:T(8,128)(2,1)} custom-call(bf16[256,512]{1,0:T(8,128)(2,1)} %tok_ref.1, f32[1,512]{1,0:T(1,128)} %bitcast.9, f32[256,128]{1,0:T(8,128)} %select_add_fusion.share_ref, bf16[2,4096,896]{2,1,0:T(8,128)(2,1)} %wg_ref.1, bf16[2,4096,896]{2,1,0:T(8,128)(2,1)} %wu_ref.1, bf16[2,896,4096]{2,1,0:T(8,128)(2,1)} %wd_ref.1, ...), custom_call_target="tpu_custom_call" | custom-call | tf_op jit(solution)/shard_map/pallas_call | solution.py:323
  104.6 1.7 %copy.14 = bf16[256,512]{1,0:T(8,128)(2,1)} copy(bf16[256,512]{1,0:T(8,128)(2,1)} %shard_map.118) | data formatting | bytes 524288
  (1 shorter events, 0.0 us)
